TPU v7x, 256 devices: a 8x8x2 block of a 8x8x16 slice. The times are simulated.
256 devices in a mesh: replica: 2 (over z), expert: 64 (over y, x), sub: 2 (over core).
Axes of the slice: x: 8, y: 8, z: 2, core: 2. Of those that a mesh axis runs over, the one named last changes fastest.
The devices are a block of a 8x8x16 slice.
Arguments:
- tokens: bfloat16 [2048, 7168], P(('replica', 'expert', 'sub')), parts along dimension 0, may hold values from -6 to 6
- expert_ids: int32 [2048, 8], P(('replica', 'expert', 'sub')), parts along dimension 0, may hold values from 0 to 31, all different within a row; in each aligned block of 8 rows (0 to 7, 8 to 15, ...) at most 3 rows name the same one
- route_levels: int32 [2048, 8], P(('replica', 'expert', 'sub')), parts along dimension 0, may hold values from 1 to 255
- gate_proj: bfloat16 [64, 7168, 512], P('expert', None, 'sub'), may hold values from -0.0625 to 0.0625
- up_proj: bfloat16 [64, 7168, 512], P('expert', None, 'sub'), may hold values from -0.0625 to 0.0625
- down_proj: bfloat16 [64, 512, 7168], P('expert', 'sub'), may hold values from -0.1875 to 0.1875
Outputs:
- moe_out: bfloat16 [2048, 7168], P(('replica', 'expert', 'sub')), parts along dimension 0
There are 2 independent parts, one for each index of `replica`. A program takes and returns all parts, laid end to end along the dimension named above; an argument that names none is the same for every part. Nothing has to cross between parts.
Inputs may be any that keep to these rules, and one draw needn't show every extreme that they name: `expert_ids`: each row names 8 different experts; among the 8 rows of one device no expert is named more than 3 times, and in some devices' rows one is named exactly 3 times.
All inputs are finite; a program needn't handle non-finite values.
Results may differ from a plain program's by a relative error of at most 0.013.
Values may be sent and summed in bfloat16 or wider, within the bound.
A program may use at most 448 MiB of HBM per device.

v0:
```python
import jax
import jax.numpy as jnp
from jax import lax
from jax.sharding import PartitionSpec as P


def local(tokens, expert_ids, route_levels, gate_proj, up_proj, down_proj):
    rows, width = tokens.shape
    experts = lax.axis_size("expert") // 2
    levels = jnp.sum(
        jnp.where(
            expert_ids[:, :, None] == jnp.arange(128, dtype=jnp.int32), route_levels[:, :, None], 0
        ),
        axis=1,
    )
    carried = jnp.concatenate([tokens, levels.astype(jnp.bfloat16)], axis=1)
    everyone = lax.all_gather(carried, ("expert", "sub"), axis=0, tiled=True)
    x = everyone[:, :width]
    level = everyone[:, width:].astype(jnp.float32)
    mine = jnp.arange(128, dtype=jnp.int32) == lax.axis_index("expert") // 2
    share = jnp.sum(jnp.where(mine, level, 0.0), axis=1, keepdims=True) / jnp.sum(
        level, axis=1, keepdims=True
    )
    gate = jnp.dot(x, gate_proj[0], preferred_element_type=jnp.float32)
    up = jnp.dot(x, up_proj[0], preferred_element_type=jnp.float32)
    hidden = (jax.nn.silu(gate) * up * share).astype(jnp.bfloat16)
    part = jnp.dot(hidden, down_proj[0], preferred_element_type=jnp.float32).astype(jnp.bfloat16)
    return lax.psum_scatter(part, ("expert", "sub"), scatter_dimension=0, tiled=True)


def solution(mesh):
    return jax.shard_map(
        local,
        mesh=mesh,
        in_specs=(
            P(("replica", "expert", "sub"), None),
            P(("replica", "expert", "sub"), None),
            P(("replica", "expert", "sub"), None),
            P("expert", None, "sub"),
            P("expert", None, "sub"),
            P("expert", "sub", None),
        ),
        out_specs=P(("replica", "expert", "sub"), None),
        check_vma=False,
    )
```

profile of v0, /device:TPU:516, one launch (start us, length us, event | category | flops | bytes accessed | tf_op | source)
XLA Modules:
  0.0 367.1 jit_solution(16336927684279294206)
XLA Ops:
  6.5 0.0 all-gather.2.cloned.1.call-start
  6.6 0.8 select_reduce_fusion
  7.4 1.5 pad_maximum_fusion
  8.9 0.1 all-gather.2.cloned.1.call-update
  9.0 0.1 reduce-scatter.2.cloned.1.call-start
  9.1 111.0 %all-gather.2.cloned.1.call-done = bf16[1024,7296]{1,0:T(8,128)(2,1)} async-done(((bf16[8,7296]{1,0:T(8,128)(2,1)}), bf16[1024,7296]{1,0:T(8,128)(2,1)}) %all-gather.2.cloned.1.call-update) | async-done | bytes 14942224 | tf_op jit(solution)/shard_map/all_gather | solution.py:17
  120.1 1.2 convert_reduce_fusion
  121.3 0.0 copy-start.1
  121.3 8.5 %fusion.2 = f32[1024,256]{1,0:T(8,128)S(1)} fusion(bf16[1024,7296]{1,0:T(8,128)(2,1)} %all-gather.2.cloned.1.call-done, bf16[1,7168,256]{2,1,0:T(8,128)(2,1)} %param.9), kind=kOutput, calls=%fused_computation.3 | convolution fusion | flops 3758096384 | bytes 19398656 | tf_op jit(solution)/shard_map/dot_general | solution.py:24
  129.8 0.0 copy-done.1
  129.8 0.0 copy-start
  129.8 9.4 %fusion.17 = bf16[1024,256]{1,0:T(8,128)(2,1)S(1)} fusion(bf16[1,7168,256]{2,1,0:T(8,128)(2,1)S(1)} %copy-done.1, bf16[1024,7296]{1,0:T(8,128)(2,1)} %all-gather.2.cloned.1.call-done, f32[1024,256]{1,0:T(8,128)S(1)} %fusion.2, f32[1024]{0:T(1024)S(1)} %div.24), kind=kOutput, calls=%fused_computation.10 | convolution fusion | flops 3759931392 | bytes 19927040 | tf_op jit(solution)/shard_map/dot_general | solution.py:25
  139.1 0.0 copy-done
  139.2 7.4 %convolution_convert_fusion = bf16[1024,7168]{1,0:T(8,128)(2,1)} fusion(bf16[1024,256]{1,0:T(8,128)(2,1)S(1)} %fusion.17, bf16[1,256,7168]{2,1,0:T(8,128)(2,1)S(1)} %copy-done), kind=kOutput, calls=%fused_computation | convolution fusion | flops 3765436416 | bytes 18874368 | tf_op jit(solution)/shard_map/dot_general | solution.py:27
  146.5 0.1 reduce-scatter.2.cloned.1.call-update
  146.6 213.6 %reduce-scatter.2.cloned.1.call-done = bf16[8,7168]{1,0:T(8,128)(2,1)} async-done(((bf16[1024,7168]{1,0:T(8,128)(2,1)}), bf16[8,7168]{1,0:T(8,128)(2,1)}) %reduce-scatter.2.cloned.1.call-update) | async-done | bytes 114704 | tf_op jit(solution)/shard_map/reduce_scatter | solution.py:28
  (3 shorter events, 0.0 us)
Async XLA Ops:
  6.5 113.5 %all-gather.2.cloned.1.call-start = ((), (), s32[]{:S(2)}) async-start(), calls=%async_computation.1 | async-start | bytes 15058944 | tf_op jit(solution)/shard_map/all_gather | solution.py:17
  9.0 351.2 %reduce-scatter.2.cloned.1.call-start = ((), (), s32[]{:S(2)}) async-start(), calls=%async_computation.2 | async-start | bytes 14794752 | tf_op jit(solution)/shard_map/reduce_scatter | solution.py:28
  121.3 8.5 %copy-start.1 = (bf16[1,7168,256]{2,1,0:T(8,128)(2,1)S(1)}, bf16[1,7168,256]{2,1,0:T(8,128)(2,1)}, u32[]{:S(2)}) copy-start(bf16[1,7168,256]{2,1,0:T(8,128)(2,1)} %param.10) | copy-start | bytes 11010052
  129.8 9.4 %copy-start = (bf16[1,256,7168]{2,1,0:T(8,128)(2,1)S(1)}, bf16[1,256,7168]{2,1,0:T(8,128)(2,1)}, u32[]{:S(2)}) copy-start(bf16[1,256,7168]{2,1,0:T(8,128)(2,1)} %param.11) | copy-start | bytes 11010052
Sparse Core Ops, SparseCore 0:
  10.0 110.0 all-gather.1
  146.7 213.4 reduce-scatter.1
where the time goes:
time: 367 us
  waiting for transfers between devices  325 us (89%)
  matrix products  25.2 us (7%)
  between operations  13.5 us (4%)
    reduce_scatter x1, waiting for transfers between devices, local(): lax.psum_scatter(part, ('expert', 'sub'), scatter_dimension=0, tiled=True)  214 us
    all_gather x1, waiting for transfers between devices, local(): everyone = lax.all_gather(carried, ('expert', 'sub'), axis=0, tiled=True)  111 us
    dot_general x1, matrix products, local(): up = jnp.dot(x, up_proj[0], preferred_element_type=jnp.float32)  9.36 us
    dot_general x1, matrix products, local(): gate = jnp.dot(x, gate_proj[0], preferred_element_type=jnp.float32)  8.45 us
    dot_general x1, matrix products, local(): jnp.dot(hidden, down_proj[0], preferred_element_type=jnp.float32)  7.38 us
  transfers between devices with their start and end apart: 2, of which 2 were waited for; matrix products, arithmetic and copies ran while one was open for 0% of the time, Pallas kernels for 0%

commit v1 on v0

--- a/solution.py
+++ b/solution.py
@@ -14,7 +14,12 @@
         axis=1,
     )
     carried = jnp.concatenate([tokens, levels.astype(jnp.bfloat16)], axis=1)
-    everyone = lax.all_gather(carried, ("expert", "sub"), axis=0, tiled=True)
+    everyone = jnp.concatenate(
+        lax.all_to_all(
+            jnp.stack([carried] * lax.axis_size(("expert", "sub"))), ("expert", "sub"), 0, 0
+        ),
+        axis=0,
+    )
     x = everyone[:, :width]
     level = everyone[:, width:].astype(jnp.float32)
     mine = jnp.arange(128, dtype=jnp.int32) == lax.axis_index("expert") // 2

time: 367 us -> 781 us (2.13)
  waiting for transfers between devices: 325 us -> 705 us
  starting transfers between devices: 0.07 us -> 27.5 us
    all_to_all x0 -> x1, waiting for transfers between devices: none -> 469 us  [local(): lax.all_to_all(jnp.stack([carried] * lax.axis_size(('expert', 'sub'))), (...]
    all_gather x1 -> x0, waiting for transfers between devices: 111 us -> none  [local(): everyone = lax.all_gather(carried, ('expert', 'sub'), axis=0, tiled=True)]
    all_to_all x0 -> x1, starting transfers between devices: none -> 27.2 us  [local(): lax.all_to_all(jnp.stack([carried] * lax.axis_size(('expert', 'sub'))), (...]
    reduce_scatter x1, waiting for transfers between devices: 214 us -> 236 us  [local(): lax.psum_scatter(part, ('expert', 'sub'), scatter_dimension=0, tiled=True)]
where the time goes in v1:
time: 781 us; the launch traced here: 780 us
  waiting for transfers between devices  705 us (90%)
  starting transfers between devices  27.5 us (4%)
  matrix products  25.2 us (3%)
  between operations  13.5 us (2%)
    all_to_all x1, waiting for transfers between devices, local(): lax.all_to_all(jnp.stack([carried] * lax.axis_size(('expert', 'sub'))), (...  469 us
    reduce_scatter x1, waiting for transfers between devices, local(): lax.psum_scatter(part, ('expert', 'sub'), scatter_dimension=0, tiled=True)  236 us
    all_to_all x1, starting transfers between devices, local(): lax.all_to_all(jnp.stack([carried] * lax.axis_size(('expert', 'sub'))), (...  27.2 us
  transfers between devices with their start and end apart: 2, of which 2 were waited for; matrix products, arithmetic and copies ran while one was open for 0% of the time, Pallas kernels for 0%

profile of v1, /device:TPU:516, one launch (start us, length us, event | category | flops | bytes accessed | tf_op | source)
XLA Modules:
  0.0 780.3 jit_solution(3678805634846786632)
XLA Ops:
  6.5 0.8 select_reduce_fusion
  7.4 0.9 pad_maximum_fusion
  8.3 6.2 stack.2
  14.5 27.2 %all-to-all-start = ((bf16[128,8,7296]{2,1,0:T(8,128)(2,1)}), bf16[128,8,7296]{2,1,0:T(8,128)(2,1)}, u32[]{:S(2)}, u32[]{:S(2)}) async-start(bf16[128,8,7296]{2,1,0:T(8,128)(2,1)} %stack.2), calls=%async_computation | async-start | bytes 29884416 | tf_op jit(solution)/shard_map/all_to_all | solution.py:18
  41.7 0.2 reduce-scatter.2.cloned.1.call-start
  42.0 469.2 %all-to-all-done = bf16[128,8,7296]{2,1,0:T(8,128)(2,1)} async-done(((bf16[128,8,7296]{2,1,0:T(8,128)(2,1)}), bf16[128,8,7296]{2,1,0:T(8,128)(2,1)}, u32[]{:S(2)}, u32[]{:S(2)}) %all-to-all-start) | async-done | bytes 14942240 | tf_op jit(solution)/shard_map/all_to_all | solution.py:18
  511.1 0.0 copy-start.1
  511.1 8.4 %fusion.2 = f32[1024,256]{1,0:T(8,128)S(1)} fusion(bf16[1024,7296]{1,0:T(8,128)(2,1)} %bitcast, bf16[1,7168,256]{2,1,0:T(8,128)(2,1)} %param.9), kind=kOutput, calls=%fused_computation.3 | convolution fusion | flops 3758096384 | bytes 19398656 | tf_op jit(solution)/shard_map/dot_general | solution.py:29
  519.6 1.2 convert_reduce_fusion
  520.8 0.0 copy-done.1
  520.8 0.0 copy-start
  520.8 9.4 %fusion.17 = bf16[1024,256]{1,0:T(8,128)(2,1)S(1)} fusion(bf16[1,7168,256]{2,1,0:T(8,128)(2,1)S(1)} %copy-done.1, bf16[1024,7296]{1,0:T(8,128)(2,1)} %bitcast, f32[1024,256]{1,0:T(8,128)S(1)} %fusion.2, f32[1024]{0:T(1024)S(1)} %div.24), kind=kOutput, calls=%fused_computation.10 | convolution fusion | flops 3759931392 | bytes 19927040 | tf_op jit(solution)/shard_map/dot_general | solution.py:30
  530.2 0.0 copy-done
  530.2 7.4 convolution_convert_fusion
  537.6 0.1 reduce-scatter.2.cloned.1.call-update
  537.6 235.8 %reduce-scatter.2.cloned.1.call-done = bf16[8,7168]{1,0:T(8,128)(2,1)} async-done(((bf16[1024,7168]{1,0:T(8,128)(2,1)}), bf16[8,7168]{1,0:T(8,128)(2,1)}) %reduce-scatter.2.cloned.1.call-update) | async-done | bytes 114704 | tf_op jit(solution)/shard_map/reduce_scatter | solution.py:33
  (3 shorter events, 0.0 us)
Async XLA Ops:
  14.5 496.7 %all-to-all-start = ((bf16[128,8,7296]{2,1,0:T(8,128)(2,1)}), bf16[128,8,7296]{2,1,0:T(8,128)(2,1)}, u32[]{:S(2)}, u32[]{:S(2)}) async-start(bf16[128,8,7296]{2,1,0:T(8,128)(2,1)} %stack.2), calls=%async_computation | async-start | bytes 29884416 | tf_op jit(solution)/shard_map/all_to_all | solution.py:18
  41.7 731.7 %reduce-scatter.2.cloned.1.call-start = ((), (), s32[]{:S(2)}) async-start(), calls=%async_computation.2 | async-start | bytes 14794752 | tf_op jit(solution)/shard_map/reduce_scatter | solution.py:33
  511.1 9.7 %copy-start.1 = (bf16[1,7168,256]{2,1,0:T(8,128)(2,1)S(1)}, bf16[1,7168,256]{2,1,0:T(8,128)(2,1)}, u32[]{:S(2)}) copy-start(bf16[1,7168,256]{2,1,0:T(8,128)(2,1)} %param.10) | copy-start | bytes 11010052
  520.8 9.4 %copy-start = (bf16[1,256,7168]{2,1,0:T(8,128)(2,1)S(1)}, bf16[1,256,7168]{2,1,0:T(8,128)(2,1)}, u32[]{:S(2)}) copy-start(bf16[1,256,7168]{2,1,0:T(8,128)(2,1)} %param.11) | copy-start | bytes 11010052
Sparse Core Ops, SparseCore 0:
  537.8 235.6 reduce-scatter.1
